TPU v7x, 32 devices: a whole 2x2x4 slice. The times are simulated.
32 devices in a mesh: gx: 4 (over z), gy: 2 (over y), gz: 4 (over x, core).
Axes of the slice: x: 2, y: 2, z: 4, core: 2. Of those that a mesh axis runs over, the one named last changes fastest.
Arguments:
- colloc: bfloat16 [768, 4000], P(('gx', 'gy')), may hold values from -6 to 6
- occ_coeffs: bfloat16 [4000, 1024], P(None, 'gz'), may hold values from -0.09375 to 0.09375
- core: bfloat16 [768, 2, 384], P('gx', 'gy'), may hold values from -6.246567e-05 to 6.246567e-05
Outputs:
- coulomb: float32 [96, 4000], P(('gx', 'gz'), 'gy')
- exchange: float32 [96, 4000], P(('gx', 'gz'), 'gy')
All inputs are finite; a program needn't handle non-finite values.
Results may differ from a plain program's by a relative error of at most 0.0089.
Values may be sent and summed in bfloat16 or wider, within the bound.
A program may use at most 64 MiB of HBM per device.

v0:
```python
import functools

import jax
import jax.numpy as jnp
import numpy as np
from jax import lax
from jax.experimental import pallas as pl
from jax.experimental.pallas import tpu as pltpu
from jax.sharding import PartitionSpec as P

W = 96
LANES = 128
DEPTH = 1024
MESH = pl.DeviceIdType.MESH
F32 = jnp.float32
BF16 = jnp.bfloat16


def up(value, step):
    return -(-value // step) * step


def dot(left, right, left_dim, right_dim):
    return lax.dot_general(
        left, right, (((left_dim,), (right_dim,)), ((), ())), preferred_element_type=F32
    )


def kernel(
    dims,
    colloc_hbm,
    coeffs_hbm,
    core_hbm,
    place_hbm,
    fold_hbm,
    out_ref,
    vals,
    coeffs,
    core,
    place,
    fold,
    cores,
    col_occ,
    row_occ,
    wins,
    win_t,
    parts,
    pot_send,
    pot_recv,
    tot_send,
    tot_recv,
    y_send,
    y_recv,
    z_send,
    z_recv,
    load_sem,
    depth_sem,
    col_sem,
    row_sem,
    win_sem,
    pot_sem,
    tot_sem,
    y_sem,
    z_sem,
):
    gx_size, gy_size, gz_size, rows, pad_rows, width, piece, tails = dims
    gx, gy, gz = lax.axis_index("gx"), lax.axis_index("gy"), lax.axis_index("gz")
    points, total = vals.shape
    band = gx_size * pad_rows
    pieces = parts.shape[1]
    slabs, _, slab = coeffs.shape

    def turn(pos, step, size):
        if size & (size - 1):
            return lax.rem(pos + step, size) if step else pos
        bit = 1
        while bit <= step:
            if step & bit:
                pos = pos + bit * (1 - 2 * lax.rem(lax.div(pos, bit), 2))
            bit *= 2
        return pos

    def peer(dx, dy, dz):
        return (turn(gx, dx, gx_size), turn(gy, dy, gy_size), turn(gz, dz, gz_size))

    loads = [
        pltpu.make_async_copy(colloc_hbm, vals, load_sem.at[0]),
        pltpu.make_async_copy(core_hbm, core, load_sem.at[1]),
        pltpu.make_async_copy(place_hbm, place, load_sem.at[2]),
        pltpu.make_async_copy(fold_hbm, fold, load_sem.at[3]),
    ]
    spans = [(s, min(DEPTH, total - s)) for s in range(0, total, DEPTH)]
    depth_loads = [
        pltpu.make_async_copy(
            coeffs_hbm.at[pl.ds(s, n), pl.ds(q * slab, slab)],
            coeffs.at[q, pl.ds(s, n)],
            depth_sem.at[q, i],
        )
        for q in range(slabs)
        for i, (s, n) in enumerate(spans)
    ]
    loads[0].start()
    for load in depth_loads:
        load.start()
    loads[1].start()
    loads[2].start()
    loads[3].start()

    barrier = pltpu.get_barrier_semaphore()
    mates = [(dx, 0, dz) for dx in range(gx_size) for dz in range(gz_size) if dx or dz]
    mates += [(0, dy, dz) for dy in range(1, gy_size) for dz in range(gz_size)]
    for mate in mates:
        pl.semaphore_signal(barrier, inc=1, device_id=peer(*mate), device_id_type=MESH)

    sent = []

    def send(src, dst, sems, out_slot, in_slot, target):
        copy = pltpu.make_async_remote_copy(
            src_ref=src,
            dst_ref=dst,
            send_sem=sems.at[(0,) + out_slot],
            recv_sem=sems.at[(1,) + in_slot],
            device_id=target,
            device_id_type=MESH,
        )
        copy.start()
        sent.append(copy)

    def arrive(dst, sems, in_slot, source):
        pltpu.make_async_remote_copy(
            src_ref=dst,
            dst_ref=dst,
            send_sem=sems.at[(0,) + in_slot],
            recv_sem=sems.at[(1,) + in_slot],
            device_id=source,
            device_id_type=MESH,
        ).wait_recv()

    loads[0].wait()
    window = vals.at[:, pl.ds(0, wins.shape[2])]
    for q in range(slabs):
        occ = jnp.zeros((points, slab), F32)
        for i, (s, n) in enumerate(spans):
            depth_loads[q * len(spans) + i].wait()
            occ += dot(vals[:, s : s + n], coeffs[q, s : s + n, :], 1, 0)
        occ = occ.astype(BF16)
        col_occ[gx, q] = occ
        row_occ[gy, q] = occ
        if q == 0:
            pl.semaphore_wait(barrier, len(mates))
        for dx in reversed(range(1, gx_size)):
            slots = (dx, q), (gx, q)
            src = col_occ.at[gx, q]
            send(src, src, col_sem, *slots, peer(dx, 0, 0))
        for dy in range(1, gy_size):
            slots = (dy, q), (gy, q)
            src = row_occ.at[gy, q]
            send(src, src, row_sem, *slots, peer(0, dy, 0))
        if q == 0:
            for dy in range(1, gy_size):
                send(window, wins.at[gy], win_sem, (dy,), (gy,), peer(0, dy, 0))

    for load in loads[1:]:
        load.wait()
    own_win = vals[:, : wins.shape[2]]
    wins[gy] = own_win
    spread = place[...]
    win_t[...] = dot(spread, own_win, 0, 1).reshape(win_t.shape)
    for a in range(gx_size):
        cores[a] = core[:, a * points : (a + 1) * points]

    def fill(h, c, u, unit):
        at = pl.ds(u * points, points)
        n = min(piece, width - unit * piece)
        s = h * width + unit * piece
        parts[h, c, at, :n] = vals[:, s : s + n]
        if n < piece:
            parts[h, c, at, n:] = jnp.zeros((points, piece - n), BF16)

    for h in range(gy_size):
        for c in range(pieces):
            fill(h, c, 0, c)
            for u in range(tails):
                fill(h, c, 1 + u, pieces + u)

    for dy in range(1, gy_size):
        slot = turn(gy, dy, gy_size)
        arrive(wins.at[slot], win_sem, (slot,), peer(0, dy, 0))
    win_rows = dot(spread, wins[...].reshape(gy_size * points, -1), 0, 1).astype(BF16)
    for dy in range(1, gy_size):
        slot = turn(gy, dy, gy_size)
        for q in range(slabs):
            arrive(row_occ.at[slot, q], row_sem, (slot, q), peer(0, dy, 0))
    row_vals = [row_occ[:, q].reshape(gy_size * points, slab) for q in range(slabs)]
    row_vals = jnp.concatenate(row_vals, axis=1)

    home = gx * gz_size + gz
    ones = jnp.ones((8, slabs * slab), BF16)
    potential = jnp.zeros((8, gy_size * points), F32)
    for dx in range(gx_size):
        a = turn(gx, dx, gx_size)
        if dx:
            for q in range(slabs):
                arrive(col_occ.at[a, q], col_sem, (a, q), peer(dx, 0, 0))
        cols = jnp.concatenate([col_occ[a, q] for q in range(slabs)], axis=1)
        core_vals = cores[a]
        gram = dot(row_vals, cols, 1, 1)
        mixed = (core_vals.astype(F32) * gram).astype(BF16)
        block = dot(win_rows, mixed, 1, 0)
        tot_send[a] = block.reshape(tot_send.shape[1:]).astype(BF16)
        for dz in range(gz_size):
            if dx or dz:
                to = peer(dx, 0, dz)
                src = tot_send.at[a, to[2]]
                out = (dx * gz_size + dz,)
                send(src, tot_recv.at[home], tot_sem, out, (home,), to)
        square = jnp.square(cols.astype(F32))
        high = square.astype(BF16)
        low = (square - high.astype(F32)).astype(BF16)
        density = dot(ones, high, 1, 1) + dot(ones, low, 1, 1)
        potential += dot(density.astype(BF16), core_vals, 1, 1)
    for h in range(gy_size):
        pot_send[h] = potential[:, h * points : (h + 1) * points]
    mine = gy * gz_size + gz
    for dy in range(gy_size):
        for dz in range(gz_size):
            if dy or dz:
                src = pot_send.at[turn(gy, dy, gy_size)]
                out = (dy * gz_size + dz,)
                send(src, pot_recv.at[mine], pot_sem, out, (mine,), peer(0, dy, dz))

    def spread_out(index, left):
        kept = []
        laid = dot(fold[...], left, 1, 0).astype(BF16).reshape(-1, band, points)
        lefts = [
            jnp.concatenate([laid[0]] + [laid[1 + c * tails + u] for u in range(tails)], axis=1)
            for c in range(pieces)
        ]
        for c in range(pieces):
            for dy in range(1, gy_size):
                h = turn(gy, dy, gy_size)
                y_send[index, c, h] = dot(lefts[c], parts[h, c], 1, 0).astype(BF16)
                slots = (index, c, dy), (index, c, gy)
                dst = y_recv.at[index, c, gy]
                send(y_send.at[index, c, h], dst, y_sem, *slots, peer(0, dy, 0))
        for c in range(pieces):
            kept.append(dot(lefts[c], parts[gy, c], 1, 0))
        return kept

    pot = pot_send[gy]
    for dy in range(gy_size):
        for dz in range(gz_size):
            if dy or dz:
                to = peer(0, dy, dz)
                slot = to[1] * gz_size + to[2]
                arrive(pot_recv.at[slot], pot_sem, (slot,), to)
                pot += pot_recv[slot]
    coul_kept = spread_out(0, (win_t[gz] * pot[:1]).astype(BF16))

    owned = tot_send[gx, gz].astype(F32)
    for dx in range(gx_size):
        for dz in range(gz_size):
            if dx or dz:
                to = peer(dx, 0, dz)
                slot = to[0] * gz_size + to[2]
                arrive(tot_recv.at[slot], tot_sem, (slot,), to)
                owned += tot_recv[slot].astype(F32)
    exch_kept = spread_out(1, owned.reshape(-1, points).astype(BF16))

    for index, kept in enumerate((coul_kept, exch_kept)):
        for c in range(pieces):
            acc = kept[c]
            for dy in range(1, gy_size):
                slot = turn(gy, dy, gy_size)
                dst = y_recv.at[index, c, slot]
                arrive(dst, y_sem, (index, c, slot), peer(0, dy, 0))
                acc += y_recv[index, c, slot].astype(F32)
            z_send[index, c] = acc.reshape(gx_size, pad_rows, piece).astype(BF16)
            for dx in range(1, gx_size):
                a = turn(gx, dx, gx_size)
                slots = (index, c, dx), (index, c, gx)
                dst = z_recv.at[index, c, gx]
                send(z_send.at[index, c, a], dst, z_sem, *slots, peer(dx, 0, 0))

    spare = pad_rows - rows
    for index in range(2):
        for c in range(pieces):
            acc = z_send[index, c, gx].astype(F32)
            for dx in range(1, gx_size):
                slot = turn(gx, dx, gx_size)
                dst = z_recv.at[index, c, slot]
                arrive(dst, z_sem, (index, c, slot), peer(dx, 0, 0))
                acc += z_recv[index, c, slot].astype(F32)
            n = min(piece, width - c * piece)
            out_ref[index, :, c * piece : c * piece + n] = acc[:rows, :n]
            for s in range(spare):
                u, r = divmod(c * spare + s, rows)
                if u < tails:
                    start = (pieces + u) * piece
                    n = min(piece, width - start)
                    line = acc[rows + s : rows + s + 1, :n]
                    out_ref[index, r : r + 1, start : start + n] = line

    for copy in sent:
        copy.wait_send()


def local(colloc, occ_coeffs, core):
    points, total = colloc.shape
    gx_size = lax.axis_size("gx")
    gy_size = lax.axis_size("gy")
    gz_size = lax.axis_size("gz")
    occupied = occ_coeffs.shape[1]
    rows = W // (gx_size * gz_size)
    pad_rows = up(rows, 8)
    width = total // gy_size
    piece = 512 if width > 512 else LANES
    units = -(-width // piece)
    spare = pad_rows - rows
    pieces = next(q for q in range(1, units + 1) if (units - q) * rows <= q * spare)
    tails = units - pieces
    row_count, flat = core.shape[0], core.shape[2]
    slab = LANES if occupied % LANES == 0 else occupied
    slabs = occupied // slab
    band = gx_size * pad_rows
    lanes = up(W, LANES)

    tight = up(gx_size * rows, 8)
    place = np.zeros((lanes, gz_size, tight), np.float32)
    for a in range(gx_size):
        for g in range(gz_size):
            for k in range(rows):
                place[(a * gz_size + g) * rows + k, g, a * rows + k] = 1
    place = jnp.asarray(place.reshape(lanes, gz_size * tight), BF16)
    fold = np.zeros((1 + pieces * tails, gx_size, pad_rows, tight), np.float32)
    for a in range(gx_size):
        for k in range(rows):
            fold[0, a, k, a * rows + k] = 1
        for c in range(pieces):
            for s in range(spare):
                u, r = divmod(c * spare + s, rows)
                if u < tails:
                    fold[1 + c * tails + u, a, rows + s, a * rows + r] = 1
    fold = jnp.asarray(fold.reshape(-1, tight), BF16)

    dims = (gx_size, gy_size, gz_size, rows, pad_rows, width, piece, tails)
    dma = pltpu.SemaphoreType.DMA
    vmem = pltpu.VMEM
    result = pl.pallas_call(
        functools.partial(kernel, dims),
        out_shape=pltpu.VMEM((2, rows, width), F32),
        in_specs=[pl.BlockSpec(memory_space=pltpu.HBM)] * 5,
        out_specs=pl.BlockSpec(memory_space=pltpu.VMEM),
        scratch_shapes=[
            vmem((points, total), BF16),
            vmem((slabs, total, slab), BF16),
            vmem((row_count, flat), BF16),
            vmem(place.shape, BF16),
            vmem(fold.shape, BF16),
            vmem((gx_size, row_count, points), BF16),
            vmem((gx_size, slabs, points, slab), BF16),
            vmem((gy_size, slabs, points, slab), BF16),
            vmem((gy_size, points, lanes), BF16),
            vmem((gz_size, tight, points), F32),
            vmem((gy_size, pieces, (1 + tails) * points, piece), BF16),
            vmem((gy_size, 8, points), F32),
            vmem((gy_size * gz_size, 8, points), F32),
            vmem((gx_size, gz_size, tight // 8, 8, points), BF16),
            vmem((gx_size * gz_size, tight // 8, 8, points), BF16),
            vmem((2, pieces, gy_size, band, piece), BF16),
            vmem((2, pieces, gy_size, band, piece), BF16),
            vmem((2, pieces, gx_size, pad_rows, piece), BF16),
            vmem((2, pieces, gx_size, pad_rows, piece), BF16),
            dma((4,)),
            dma((slabs, -(-total // DEPTH))),
            dma((2, gx_size, slabs)),
            dma((2, gy_size, slabs)),
            dma((2, gy_size)),
            dma((2, gy_size * gz_size)),
            dma((2, gx_size * gz_size)),
            dma((2, 2, pieces, gy_size)),
            dma((2, 2, pieces, gx_size)),
        ],
        compiler_params=pltpu.CompilerParams(
            collective_id=0, has_side_effects=True, vmem_limit_bytes=60 * 1024 * 1024
        ),
    )(colloc, occ_coeffs, core.reshape(row_count, flat), place, fold)
    return result[0], result[1]


def solution(mesh):
    in_specs = (P(("gx", "gy"), None), P(None, "gz"), P("gx", "gy", None))
    out_specs = (P(("gx", "gz"), "gy"), P(("gx", "gz"), "gy"))
    return jax.shard_map(local, mesh=mesh, in_specs=in_specs, out_specs=out_specs, check_vma=False)
```

profile of v0, /device:TPU:0, one launch (start us, length us, event | category | flops | bytes accessed | tf_op | source)
XLA Modules:
  0.0 29.1 jit_solution(13869520751816835915)
XLA Ops:
  0.6 27.8 %shard_map.68 = f32[2,6,2000]{2,1,0:T(8,128)S(1)} custom-call(bf16[96,4000]{1,0:T(8,128)(2,1)} %colloc_hbm.1, bf16[4000,256]{1,0:T(8,128)(2,1)} %coeffs_hbm.1, bf16[192,384]{1,0:T(8,128)(2,1)} %bitcast.5, bf16[128,96]{1,0:T(8,128)(2,1)} %constant.4.clone.place_hbm, bf16[128,24]{1,0:T(8,128)(2,1)} %constant.5.clone.fold_hbm), custom_call_target="tpu_custom_call" | custom-call | tf_op jit(solution)/shard_map/pallas_call | solution.py:349
  28.4 0.7 %slice_bitcast_fusion = (f32[6,2000]{1,0:T(8,128)}, f32[6,2000]{1,0:T(8,128)}) fusion(f32[2,6,2000]{2,1,0:T(8,128)S(1)} %shard_map.68), kind=kLoop, calls=%fused_computation | loop fusion | bytes 192000 | tf_op jit(solution)/shard_map/squeeze | solution.py:388
where the time goes:
time: 29.3 us; the launch traced here: 29.1 us
  Pallas kernels  27.8 us (95%)
  local copies, waits for them, and re-layouts  0.66 us (2%)
  between operations  0.64 us (2%)
    pallas_call x1, Pallas kernels, local(): pl.pallas_call(functools.partial(kernel, dims), out_shape=pltpu.VMEM((2,...  27.8 us
    squeeze x1, local copies, waits for them, and re-layouts, local(): return (result[0], result[1])  0.66 us

commit v1 on v0

v1 whole, which is shorter than its diff:
```python
import functools

import jax
import jax.numpy as jnp
import numpy as np
from jax import lax
from jax.experimental import pallas as pl
from jax.experimental.pallas import tpu as pltpu
from jax.sharding import PartitionSpec as P

W = 96
LANES = 128
DEPTH = 1024
MESH = pl.DeviceIdType.MESH
F32 = jnp.float32
BF16 = jnp.bfloat16


def up(value, step):
    return -(-value // step) * step


def dot(left, right, left_dim, right_dim):
    return lax.dot_general(
        left, right, (((left_dim,), (right_dim,)), ((), ())), preferred_element_type=F32
    )


def kernel(
    dims,
    colloc_hbm,
    coeffs_hbm,
    core_hbm,
    place_hbm,
    out_ref,
    vals,
    coeffs,
    core,
    place,
    cores,
    core_t,
    row_occ,
    col_occ,
    row_win,
    col_win,
    win_t,
    dens,
    stage,
    cols,
    pot_send,
    pot_recv,
    tot_send,
    tot_recv,
    z_send,
    z_recv,
    load_sem,
    depth_sem,
    ready,
    core_sem,
    core_fwd_sem,
    row_sem,
    col_sem,
    row_win_sem,
    row_win_fwd_sem,
    col_win_sem,
    dens_sem,
    cols_sem,
    cols_fwd_sem,
    pot_sem,
    tot_sem,
    z_sem,
):
    gx_size, gy_size, gz_size, rows, width = dims
    gx, gy, gz = lax.axis_index("gx"), lax.axis_index("gy"), lax.axis_index("gz")
    points, total = vals.shape
    lanes = row_win.shape[3]
    halves, half = row_win.shape[1], row_win.shape[2]
    span = cols.shape[2]
    side = gy_size * points
    part = lax.rem(gz, halves)

    def turn(pos, step, size):
        if size & (size - 1):
            return lax.rem(pos + step, size) if step else pos
        bit = 1
        while bit <= step:
            if step & bit:
                pos = pos + bit * (1 - 2 * lax.rem(lax.div(pos, bit), 2))
            bit *= 2
        return pos

    planes = [turn(gx, d, gx_size) for d in range(1, gx_size)]
    sides = [turn(gy, d, gy_size) for d in range(1, gy_size)]
    flat = [
        (turn(gy, dy, gy_size), turn(gz, dz, gz_size))
        for dy in range(gy_size)
        for dz in range(gz_size)
        if dy or dz
    ]
    mate = (gx, gy, turn(gz, 1, gz_size))

    def copy(src, dst, sems, out_slot, in_slot, target):
        return pltpu.make_async_remote_copy(
            src_ref=src,
            dst_ref=dst,
            send_sem=sems.at[(0,) + out_slot],
            recv_sem=sems.at[(1,) + in_slot],
            device_id=target,
            device_id_type=MESH,
        )

    def arrive(dst, sems, in_slot):
        copy(dst, dst, sems, in_slot, in_slot, mate).wait_recv()

    def core_copy(t, h):
        whole = cores.at[t, h], core_t.at[gx, :, gy]
        return copy(*whole, core_sem, (t, h), (gx, gy), (t, h, gz))

    def core_part_copy(t, h):
        some = cores.at[t, h, part], core_t.at[gx, part, gy]
        return copy(*some, core_sem, (t, h), (gx, gy), (t, h, gz))

    def core_fwd(z):
        some = core_t.at[z, part]
        return copy(some, some, core_fwd_sem, (z,), (z,), mate)

    def row_win_copy(t):
        src = vals.at[pl.ds(pl.multiple_of(part * half, half), half), pl.ds(0, lanes)]
        return copy(src, row_win.at[gx, part], row_win_sem, (t,), (gx,), (t, gy, gz))

    def row_win_fwd(z):
        some = row_win.at[z, part]
        return copy(some, some, row_win_fwd_sem, (z,), (z,), mate)

    def col_win_copy(h):
        src = vals.at[:, pl.ds(0, lanes)]
        return copy(src, col_win.at[gy], col_win_sem, (h,), (gy,), (gx, h, gz))

    def dens_copy(t):
        some = dens.at[gx]
        return copy(some, some, dens_sem, (t,), (gx,), (t, gy, gz))

    def row_copy(t):
        some = row_occ.at[gx]
        return copy(some, some, row_sem, (t,), (gx,), (t, gy, gz))

    def col_copy(h):
        some = col_occ.at[gy]
        return copy(some, some, col_sem, (h,), (gy,), (gx, h, gz))

    def cols_copy(h):
        at = pl.ds(pl.multiple_of(part * half, half), half)
        return copy(stage.at[h, at], cols.at[gy, at], cols_sem, (h,), (gy,), (gx, h, gz))

    def cols_fwd(h):
        some = cols.at[h, pl.ds(pl.multiple_of(part * half, half), half)]
        return copy(some, some, cols_fwd_sem, (h,), (h,), mate)

    mine = gy * gz_size + gz

    def pot_copy(h, g):
        return copy(pot_send, pot_recv.at[mine], pot_sem, (h * gz_size + g,), (mine,), (gx, h, g))

    def tot_copy(h, g):
        slots = (h * gz_size + g,), (mine,)
        return copy(tot_send.at[g], tot_recv.at[mine], tot_sem, *slots, (gx, h, g))

    def z_copy(index, t):
        dst = z_recv.at[index, gx]
        return copy(z_send.at[index, t], dst, z_sem, (index, t), (index, gx), (t, gy, gz))

    load_core = pltpu.make_async_copy(core_hbm, core, load_sem.at[0])
    load_vals = pltpu.make_async_copy(colloc_hbm, vals, load_sem.at[1])
    load_place = pltpu.make_async_copy(place_hbm, place, load_sem.at[2])
    spans = [(s, min(DEPTH, total - s)) for s in range(0, total, DEPTH)]
    depth_loads = [
        pltpu.make_async_copy(
            coeffs_hbm.at[pl.ds(s, n)], coeffs.at[pl.ds(s, n)], depth_sem.at[i]
        )
        for i, (s, n) in enumerate(spans)
    ]
    load_core.start()
    load_vals.start()
    for load in depth_loads:
        load.start()
    load_place.start()

    barrier = pltpu.get_barrier_semaphore()
    for h, g in flat:
        pl.semaphore_signal(barrier, inc=1, device_id=(gx, h, g), device_id_type=MESH)
    for t in range(1, gx_size):

        @pl.when(gx < t)
        def _():
            for h in range(gy_size):
                pl.semaphore_signal(barrier, inc=1, device_id=(t, h, gz), device_id_type=MESH)

    load_core.wait()
    for a in range(gx_size):
        block = core[:, a * points : (a + 1) * points]
        cores[a] = block.reshape(cores.shape[1:])

    pl.semaphore_wait(barrier, len(flat) + gx * gy_size)
    for t in range(gx_size - 1):

        @pl.when(gx > t)
        def _():
            for h in range(gy_size):
                pl.semaphore_signal(
                    ready.at[gx], inc=1, device_id=(t, h, gz), device_id_type=MESH
                )
            for h in range(gy_size):
                core_part_copy(t, h).start()

    for h in sides:
        core_copy(gx, h).start()
    core_t[gx, :, gy] = cores[gx, gy]

    load_vals.wait()
    for t in range(gx_size - 1):

        @pl.when(gx > t)
        def _():
            row_win_copy(t).start()

    for h in sides:
        col_win_copy(h).start()
    for h in range(gy_size):
        stage[h, :, :width] = vals[:, h * width : (h + 1) * width]
        if width < span:
            stage[h, :, width:] = jnp.zeros((points, span - width), BF16)
    own_cols = pltpu.make_async_copy(stage.at[gy], cols.at[gy], load_sem.at[3])

    occ = jnp.zeros((points, coeffs.shape[1]), F32)
    for i, (s, n) in enumerate(spans):
        depth_loads[i].wait()
        occ += dot(vals[:, s : s + n], coeffs[s : s + n, :], 1, 0)
    occ = occ.astype(BF16)
    row_occ[gx] = occ
    col_occ[gy] = occ
    square = jnp.square(occ.astype(F32))
    high = square.astype(BF16)
    low = (square - high.astype(F32)).astype(BF16)
    ones = jnp.ones((8, occ.shape[1]), BF16)
    dens[gx] = dot(ones, high, 1, 1) + dot(ones, low, 1, 1)
    for t in range(gx_size - 1):

        @pl.when(gx > t)
        def _():
            dens_copy(t).start()
            row_copy(t).start()

    for h in sides:
        col_copy(h).start()
    for h in sides:
        cols_copy(h).start()
    own_cols.start()
    for t in range(1, gx_size):

        @pl.when(gx < t)
        def _():
            pl.semaphore_wait(ready.at[t], gy_size)
            for h in range(gy_size):
                core_part_copy(t, h).start()
            dens_copy(t).start()
            row_win_copy(t).start()
            row_copy(t).start()

    own_win = vals[:, :lanes]
    row_win[gx] = own_win.reshape(row_win.shape[1:])
    col_win[gy] = own_win
    load_place.wait()
    spread = place[...]

    for z in planes:
        for h in range(gy_size):
            arrive(core_t.at[z, part, h], core_sem, (z, h))
        if halves > 1:
            core_fwd(z).start()
        arrive(row_win.at[z, part], row_win_sem, (z,))
        if halves > 1:
            row_win_fwd(z).start()

    def potential_of(z):
        return dot(dens[z].astype(BF16), cores[z].reshape(side, points), 1, 1)

    potential = potential_of(gx)
    for z in planes:
        arrive(dens.at[z], dens_sem, (z,))
        potential += potential_of(z)
    pot_send[...] = potential
    for h, g in flat:
        pot_copy(h, g).start()

    for h in sides:
        arrive(core_t.at[gx, :, h], core_sem, (gx, h))
        arrive(col_win.at[h], col_win_sem, (h,))
        arrive(col_occ.at[h], col_sem, (h,))
    win_t[...] = dot(spread, col_win[...].reshape(side, lanes), 0, 1).reshape(win_t.shape)
    col_vals = col_occ[...].reshape(side, col_occ.shape[2])

    block = None
    for i, z in enumerate([gx] + planes):
        if i:
            if halves > 1:
                other = 1 - part
                arrive(core_t.at[z, other], core_fwd_sem, (z,))
                arrive(row_win.at[z, other], row_win_fwd_sem, (z,))
            arrive(row_occ.at[z], row_sem, (z,))
        win_rows = dot(spread, row_win[z].reshape(points, lanes), 0, 1).astype(BF16)
        gram = dot(row_occ[z], col_vals, 1, 1)
        core_vals = jnp.concatenate(
            [core_t[z, :, h].reshape(points, points) for h in range(gy_size)], axis=1
        )
        mixed = (core_vals.astype(F32) * gram).astype(BF16)
        term = dot(win_rows, mixed, 1, 0)
        block = term if block is None else block + term
    tot_send[...] = block.reshape(tot_send.shape).astype(BF16)
    for h, g in flat:
        tot_copy(h, g).start()

    for h in sides:
        at = pl.ds(pl.multiple_of(part * half, half), half)
        arrive(cols.at[h, at], cols_sem, (h,))
        if halves > 1:
            cols_fwd(h).start()

    def spread_out(index, left):
        spare = jnp.zeros((8 - rows, side), F32)
        lines = []
        for a in range(gx_size):
            lines += [left[a * rows : (a + 1) * rows], spare]
        lefts = jnp.concatenate(lines, axis=0).astype(BF16)
        out = dot(lefts, cols[...].reshape(side, span), 1, 0)
        z_send[index] = out.reshape(gx_size, 8, span).astype(BF16)
        for t in planes[::-1]:
            z_copy(index, t).start()

    pot = pot_send[...]
    for h, g in flat:
        slot = h * gz_size + g
        arrive(pot_recv.at[slot], pot_sem, (slot,))
        pot += pot_recv[slot]
    weighted = (win_t[gz] * pot[:1]).astype(BF16).astype(F32)
    own_cols.wait()
    if halves > 1:
        for h in sides:
            at = pl.ds(pl.multiple_of((1 - part) * half, half), half)
            arrive(cols.at[h, at], cols_fwd_sem, (h,))
    spread_out(0, weighted)

    owned = tot_send[gz].astype(F32)
    for h, g in flat:
        slot = h * gz_size + g
        arrive(tot_recv.at[slot], tot_sem, (slot,))
        owned += tot_recv[slot].astype(F32)
    tight = win_t.shape[1]
    owned = owned.reshape(-1, side)[:tight]
    spread_out(1, owned)

    for index in range(2):
        acc = z_send[index, gx].astype(F32)
        for z in planes:
            arrive(z_recv.at[index, z], z_sem, (index, z))
            acc += z_recv[index, z].astype(F32)
        out_ref[index] = acc[:rows, :width]

    for h in sides:
        core_copy(gx, h).wait_send()
        col_win_copy(h).wait_send()
        col_copy(h).wait_send()
        cols_copy(h).wait_send()
        if halves > 1:
            cols_fwd(h).wait_send()
    for t in planes:
        for h in range(gy_size):
            core_part_copy(t, h).wait_send()
        row_win_copy(t).wait_send()
        dens_copy(t).wait_send()
        row_copy(t).wait_send()
        if halves > 1:
            core_fwd(t).wait_send()
            row_win_fwd(t).wait_send()
        for index in range(2):
            z_copy(index, t).wait_send()
    for h, g in flat:
        pot_copy(h, g).wait_send()
        tot_copy(h, g).wait_send()


def local(colloc, occ_coeffs, core):
    points, total = colloc.shape
    gx_size = lax.axis_size("gx")
    gy_size = lax.axis_size("gy")
    gz_size = lax.axis_size("gz")
    occupied = occ_coeffs.shape[1]
    rows = W // (gx_size * gz_size)
    width = total // gy_size
    row_count, flat = core.shape[0], core.shape[2]
    lanes = up(W, LANES)
    side = gy_size * points
    span = up(width, LANES)
    halves = 2 if gz_size % 2 == 0 else 1
    half = points // halves

    used = gx_size * rows
    tight = up(used, 8)
    place = np.zeros((lanes, gz_size, tight), np.float32)
    for a in range(gx_size):
        for g in range(gz_size):
            for k in range(rows):
                place[(a * gz_size + g) * rows + k, g, a * rows + k] = 1
    place = jnp.asarray(place.reshape(lanes, gz_size * tight), BF16)

    dims = (gx_size, gy_size, gz_size, rows, width)
    dma = pltpu.SemaphoreType.DMA
    vmem = pltpu.VMEM
    result = pl.pallas_call(
        functools.partial(kernel, dims),
        out_shape=pltpu.VMEM((2, rows, width), F32),
        in_specs=[pl.BlockSpec(memory_space=pltpu.HBM)] * 4,
        out_specs=pl.BlockSpec(memory_space=pltpu.VMEM),
        scratch_shapes=[
            vmem((points, total), BF16),
            vmem((total, occupied), BF16),
            vmem((row_count, flat), BF16),
            vmem(place.shape, BF16),
            vmem((gx_size, gy_size, halves, half, points), BF16),
            vmem((gx_size, halves, gy_size, half, points), BF16),
            vmem((gx_size, points, occupied), BF16),
            vmem((gy_size, points, occupied), BF16),
            vmem((gx_size, halves, half, lanes), BF16),
            vmem((gy_size, points, lanes), BF16),
            vmem((gz_size, tight, side), F32),
            vmem((gx_size, 8, points), F32),
            vmem((gy_size, points, span), BF16),
            vmem((gy_size, points, span), BF16),
            vmem((8, side), F32),
            vmem((gy_size * gz_size, 8, side), F32),
            vmem((gz_size, tight // 8, 8, side), BF16),
            vmem((gy_size * gz_size, tight // 8, 8, side), BF16),
            vmem((2, gx_size, 8, span), BF16),
            vmem((2, gx_size, 8, span), BF16),
            dma((4,)),
            dma((-(-total // DEPTH),)),
            pltpu.SemaphoreType.REGULAR((gx_size,)),
            dma((2, gx_size, gy_size)),
            dma((2, gx_size)),
            dma((2, gx_size)),
            dma((2, gy_size)),
            dma((2, gx_size)),
            dma((2, gx_size)),
            dma((2, gy_size)),
            dma((2, gx_size)),
            dma((2, gy_size)),
            dma((2, gy_size)),
            dma((2, gy_size * gz_size)),
            dma((2, gy_size * gz_size)),
            dma((2, 2, gx_size)),
        ],
        compiler_params=pltpu.CompilerParams(
            collective_id=0, has_side_effects=True, vmem_limit_bytes=60 * 1024 * 1024
        ),
    )(colloc, occ_coeffs, core.reshape(row_count, flat), place)
    return result[0], result[1]


def solution(mesh):
    in_specs = (P(("gx", "gy"), None), P(None, "gz"), P("gx", "gy", None))
    out_specs = (P(("gx", "gz"), "gy"), P(("gx", "gz"), "gy"))
    return jax.shard_map(local, mesh=mesh, in_specs=in_specs, out_specs=out_specs, check_vma=False)
```

time: 29.3 us -> 28.5 us (0.973)
  Pallas kernels: 27.8 us -> 27 us
    pallas_call x1, Pallas kernels: 27.8 us -> 27 us  [local(): pl.pallas_call(functools.partial(kernel, dims), out_shape=pltpu.VMEM((2,...]
where the time goes in v1:
time: 28.5 us; the launch traced here: 28.3 us
  Pallas kernels  27 us (95%)
  local copies, waits for them, and re-layouts  0.66 us (2%)
  between operations  0.64 us (2%)
    pallas_call x1, Pallas kernels, local(): pl.pallas_call(functools.partial(kernel, dims), out_shape=pltpu.VMEM((2,...  27 us
    squeeze x1, local copies, waits for them, and re-layouts, local(): return (result[0], result[1])  0.66 us

profile of v1, /device:TPU:0, one launch (start us, length us, event | category | flops | bytes accessed | tf_op | source)
XLA Modules:
  0.0 28.3 jit_solution(14194622625660255660)
XLA Ops:
  0.6 27.0 %shard_map.59 = f32[2,6,2000]{2,1,0:T(8,128)S(1)} custom-call(bf16[96,4000]{1,0:T(8,128)(2,1)} %colloc_hbm.1, bf16[4000,256]{1,0:T(8,128)(2,1)} %coeffs_hbm.1, bf16[192,384]{1,0:T(8,128)(2,1)} %bitcast.5, bf16[128,96]{1,0:T(8,128)(2,1)} %constant.2.clone.place_hbm), custom_call_target="tpu_custom_call" | custom-call | tf_op jit(solution)/shard_map/pallas_call | solution.py:418
  27.7 0.7 %slice_bitcast_fusion = (f32[6,2000]{1,0:T(8,128)}, f32[6,2000]{1,0:T(8,128)}) fusion(f32[2,6,2000]{2,1,0:T(8,128)S(1)} %shard_map.59), kind=kLoop, calls=%fused_computation | loop fusion | bytes 192000 | tf_op jit(solution)/shard_map/squeeze | solution.py:465
